TPU v7x, 32 devices: a whole 2x2x4 slice. The times are simulated.
32 devices in a mesh: grp: 2 (over y), row: 4 (over z), head: 2 (over x), br: 2 (over core).
Axes of the slice: x: 2, y: 2, z: 4, core: 2. Of those that a mesh axis runs over, the one named last changes fastest.
Arguments:
- pair_acts: float32 [16, 8, 128], P(('grp', 'row', 'head')), parts along dimension 0, may hold values from -6 to 6
- alignment: float32 [64, 8, 256], P(('grp', 'br'), ('row', 'head')), parts along dimension 0, may hold values from -6 to 6
- align_mask: int32 [64, 8], P('grp', ('row', 'head')), parts along dimension 0, may hold values from 0 to 1
- residue_mask: int32 [16], P('grp'), parts along dimension 0, may hold values from 0 to 1, as said below
- align_gain: float32 [256], replicated, may hold values from 0.25 to 1.75
- outer_in: float32 [256, 64], replicated, may hold values from -0.375 to 0.375
- outer_out: float32 [1024, 128], replicated, may hold values from -1 to 1
- tri_gain: float32 [2, 128], replicated, may hold values from 0.25 to 1.75
- tri_in: float32 [2, 128, 4, 128], P(None, None, 'br'), may hold values from -5 to 5
- tri_bias: float32 [2, 128, 4], P(None, None, 'br'), may hold values from -0.5 to 0.5
- tri_out: float32 [2, 4, 32, 128], P(None, 'br'), may hold values from -0.5 to 0.5
- pair_cotangent: float32 [16, 8, 128], P(('grp', 'row', 'head')), parts along dimension 0, may hold values from -6 to 6
Outputs:
- pair_out: float32 [16, 8, 128], P(('grp', 'row', 'head')), parts along dimension 0
- pair_grad: float32 [16, 8, 128], P(('grp', 'row', 'head')), parts along dimension 0
There are 2 independent parts, one for each index of `grp`. A program takes and returns all parts, laid end to end along the dimension named above; an argument that names none is the same for every part. Nothing has to cross between parts.
Inputs may be any that keep to these rules, and one draw needn't show every extreme that they name: `residue_mask`: 1 at residue 0, and 0 at one or more residues; `align_mask`: 1 at every residue of sequence 0 of each part.
All inputs are finite; a program needn't handle non-finite values.
Results may differ from a plain program's by a relative error of at most 0.0003.
Values sent between devices are 32-bit elements; how exact they have to be, the bound alone decides.
No kernel may reach another device: no remote copies, remote signals or barrier semaphores. Data moves between devices by JAX's collectives and lax.ppermute only.
A program may use at most 64 MiB of HBM per device.

v0:
```python
import jax
import jax.numpy as jnp
from jax import lax
from jax.sharding import PartitionSpec as P

OPC = 32
PRECISE = lax.Precision.HIGHEST
EPSILON = 1e-05
MASK_SHIFT = 1000000000.0


def normalize(values, scales):
    average = jnp.mean(values, axis=-1, keepdims=True)
    centred = values - average
    spread = jnp.mean(centred * centred, axis=-1, keepdims=True)
    return centred * lax.rsqrt(spread + EPSILON) * scales


def core_total(values):
    return lax.psum(values, "br")


def reorient(values):
    turned = jnp.swapaxes(values, 0, 1)
    return lax.all_to_all(turned, ("row", "head"), split_axis=0, concat_axis=1, tiled=True)


def prepare(values, scales, weight_in, weight_bias):
    normed = normalize(values, scales)
    projected = jnp.einsum("ijc,chd->ijhd", normed, weight_in, precision=PRECISE)
    bias_local = jnp.einsum("jkc,ch->hjk", normed, weight_bias, precision=PRECISE)
    return (projected, bias_local)


def attend(projected, bias_full, key_shift, weight_out):
    head_size = projected.shape[-1] // 4
    queries = projected[..., :head_size]
    key_proj = projected[..., head_size : 2 * head_size]
    value_proj = projected[..., 2 * head_size : 3 * head_size]
    gating = projected[..., 3 * head_size :]
    logits = jnp.einsum("ijhd,ikhd->ihjk", queries, key_proj, precision=PRECISE) * head_size ** (
        -0.5
    )
    logits = logits + bias_full[None] + key_shift
    attention = jax.nn.softmax(logits, axis=-1)
    attended = jnp.einsum("ihjk,ikhd->ijhd", attention, value_proj, precision=PRECISE)
    gated_out = jax.nn.sigmoid(gating) * attended
    return jnp.einsum("ijhd,hdc->ijc", gated_out, weight_out, precision=PRECISE)


def tri_forward(rows_in, scales, weight_in, weight_bias, weight_out, key_shift, pair_mask):

    def local_prep(values):
        return prepare(values, scales, weight_in, weight_bias)

    (projected, bias_local), pull_prep = jax.vjp(local_prep, rows_in)
    bias_full = lax.all_gather(bias_local, ("row", "head"), axis=1, tiled=True)

    def local_attend(proj_in, bias_in):
        return attend(proj_in, bias_in, key_shift, weight_out)

    partial_out, pull_attend = jax.vjp(local_attend, projected, bias_full)
    total_out = core_total(partial_out)
    return (rows_in + total_out * pair_mask, (pull_prep, pull_attend))


def tri_backward(grad_out, saved, pair_mask):
    pull_prep, pull_attend = saved
    grad_proj, grad_bias = pull_attend(grad_out * pair_mask)
    grad_local = lax.psum_scatter(grad_bias, ("row", "head"), scatter_dimension=1, tiled=True)
    (grad_rows,) = pull_prep((grad_proj, grad_local))
    return grad_out + core_total(grad_rows)


def body(
    pair_acts,
    alignment,
    align_mask,
    residue_mask,
    align_gain,
    outer_in,
    outer_out,
    tri_gain,
    tri_in,
    tri_bias,
    tri_out,
    pair_cotangent,
):
    row_count = pair_acts.shape[0]
    live = residue_mask.astype(jnp.float32)
    key_shift = (live - 1.0) * MASK_SHIFT
    row_live = lax.dynamic_slice_in_dim(
        live, lax.axis_index(("row", "head")) * row_count, row_count, 0
    )
    pair_mask = row_live[:, None, None] * live[None, :, None]
    seq_count = alignment.shape[0]
    mask_all = align_mask.astype(jnp.float32)
    mask_own = lax.dynamic_slice_in_dim(mask_all, lax.axis_index("br") * seq_count, seq_count, 0)
    normed = normalize(alignment, align_gain)
    projected = jnp.einsum("snc,ck->snk", normed, outer_in, precision=PRECISE)
    left_part = projected[..., :OPC] * mask_own[..., None]
    right_part = jnp.swapaxes(projected[..., OPC:] * mask_own[..., None], 1, 2)
    right_all, mask_cols = (
        lax.all_gather(right_part, ("row", "head"), axis=2, tiled=True),
        lax.all_gather(mask_all, ("row", "head"), axis=1, tiled=True),
    )
    counts = jnp.einsum("si,sj->ij", mask_all, mask_cols, precision=PRECISE)
    table = outer_out.reshape(OPC, OPC, outer_out.shape[-1])
    mixed_left = jnp.einsum("sip,pqc->siqc", left_part, table, precision=PRECISE)
    partial_outer = jnp.einsum("siqc,sqj->ijc", mixed_left, right_all, precision=PRECISE)
    outer_sum = core_total(partial_outer)
    pair_one = pair_acts + outer_sum / counts[..., None]
    pair_two, saved_start = tri_forward(
        pair_one, tri_gain[0], tri_in[0], tri_bias[0], tri_out[0], key_shift, pair_mask
    )
    turned_two = reorient(pair_two)
    turned_three, saved_end = tri_forward(
        turned_two, tri_gain[1], tri_in[1], tri_bias[1], tri_out[1], key_shift, pair_mask
    )
    pair_out = reorient(turned_three)
    grad_turned = reorient(pair_cotangent)
    grad_turned = tri_backward(grad_turned, saved_end, pair_mask)
    grad_two = reorient(grad_turned)
    pair_grad = tri_backward(grad_two, saved_start, pair_mask)
    return (pair_out, pair_grad)


def solution(mesh):
    in_specs = (
        P(("grp", "row", "head"), None, None),
        P(("grp", "br"), ("row", "head"), None),
        P("grp", ("row", "head")),
        P("grp"),
        P(),
        P(),
        P(),
        P(),
        P(None, None, "br", None),
        P(None, None, "br"),
        P(None, "br", None, None),
        P(("grp", "row", "head"), None, None),
    )
    out_specs = (P(("grp", "row", "head"), None, None), P(("grp", "row", "head"), None, None))
    return jax.shard_map(body, mesh=mesh, in_specs=in_specs, out_specs=out_specs, check_vma=False)
```

profile of v0, /device:TPU:0, one launch (start us, length us, event | category | flops | bytes accessed | tf_op | source)
XLA Modules:
  0.0 188.4 jit_solution(10134027815885279675)
XLA Ops:
  0.7 1.0 reduce_sum.121
  2.0 0.7 convert_bitcast_fusion
  2.6 0.8 multiply_multiply_fusion
  3.7 32.3 %all_gather.12 = f32[16,32,8]{1,0,2:T(8,128)S(1)} all-gather(f32[16,32,1]{1,0,2:T(8,128)S(1)} %fusion.30), channel_id=1, replica_groups=mesh['grp'=2,'row'=4,'head'=2,'br'=2] {'row','head'}, dimensions={2}, use_global_device_ids=true | all-gather | bytes 18432 | tf_op jit(solution)/shard_map/all_gather | solution.py:104
  36.9 0.7 convolution_bitcast_fusion.17
  37.6 2.5 %psum.35 = f32[1,8,128]{2,1,0:T(8,128)S(1)} all-reduce(f32[1,8,128]{2,1,0:T(8,128)S(1)} %convolution_bitcast_fusion.17), channel_id=1, replica_groups=mesh['grp'=2,'row'=4,'head'=2,'br'=2] {'br'}, use_global_device_ids=true, to_apply=%region_2.0 | all-reduce | flops 1024 | bytes 8192 | tf_op jit(solution)/shard_map/psum | solution.py:20
  40.0 20.4 %all-gather.2 = f32[8,1,32]{2,1,0:T(1,128)S(1)} all-gather(f32[1,1,32]{2,1,0:T(1,128)S(1)} %get-tuple-element.16), channel_id=1, replica_groups=mesh['grp'=2,'row'=4,'head'=2,'br'=2] {'row','head'}, dimensions={0}, use_global_device_ids=true | all-gather | bytes 1152 | tf_op jit(solution)/shard_map/all_gather | solution.py:105
  65.1 16.3 %all-gather.3 = f32[8,8,2]{1,2,0:T(2,128)S(1)} all-gather(f32[1,8,2]{1,2,0:T(2,128)S(1)} %convolution_bitcast_fusion.19), channel_id=2, replica_groups=mesh['grp'=2,'row'=4,'head'=2,'br'=2] {'row','head'}, dimensions={0}, use_global_device_ids=true | all-gather | bytes 576 | tf_op jit(solution)/shard_map/all_gather | solution.py:57
  82.8 2.5 %psum.36 = f32[1,8,128]{2,1,0:T(8,128)S(1)} all-reduce(f32[1,8,128]{2,1,0:T(8,128)S(1)} %convolution_bitcast_fusion.16), channel_id=1, replica_groups=mesh['grp'=2,'row'=4,'head'=2,'br'=2] {'br'}, use_global_device_ids=true, to_apply=%region_7.0 | all-reduce | flops 1024 | bytes 8192 | tf_op jit(solution)/shard_map/psum | solution.py:20
  85.2 0.7 multiply_add_fusion
  85.9 3.3 %all-to-all-start = ((f32[8,1,128]{2,1,0:T(1,128)}), f32[8,1,128]{2,1,0:T(1,128)S(1)}, u32[]{:S(2)}, u32[]{:S(2)}) async-start(f32[8,1,128]{2,1,0:T(1,128)} %bitcast.32), calls=%async_computation | async-start | bytes 8192 | tf_op jit(solution)/shard_map/all_to_all | solution.py:25
  90.5 5.1 %all-to-all-done = f32[8,1,128]{2,1,0:T(1,128)S(1)} async-done(((f32[8,1,128]{2,1,0:T(1,128)}), f32[8,1,128]{2,1,0:T(1,128)S(1)}, u32[]{:S(2)}, u32[]{:S(2)}) %all-to-all-start) | async-done | bytes 4128 | tf_op jit(solution)/shard_map/all_to_all | solution.py:25
  95.6 3.3 %all-to-all-start.2 = ((f32[8,1,128]{2,1,0:T(1,128)}), f32[8,1,128]{2,1,0:T(1,128)S(1)}, u32[]{:S(2)}, u32[]{:S(2)}) async-start(f32[8,1,128]{2,1,0:T(1,128)} %bitcast.54), calls=%async_computation.2 | async-start | bytes 8192 | tf_op jit(solution)/shard_map/all_to_all | solution.py:25
  99.5 20.9 %all-gather.4 = f32[8,8,2]{1,2,0:T(2,128)S(1)} all-gather(f32[1,8,2]{1,2,0:T(2,128)S(1)} %convolution_bitcast_fusion.18), channel_id=3, replica_groups=mesh['grp'=2,'row'=4,'head'=2,'br'=2] {'row','head'}, dimensions={0}, use_global_device_ids=true | all-gather | bytes 576 | tf_op jit(solution)/shard_map/all_gather | solution.py:57
  122.7 17.4 %all-reduce.8 = f32[2,8,8]{2,0,1:T(2,128)S(1)} all-reduce(f32[2,8,8]{2,0,1:T(2,128)S(1)} %copy.49), channel_id=4, replica_groups=mesh['grp'=2,'row'=4,'head'=2,'br'=2] {'row','head'}, use_global_device_ids=true, to_apply=%region_14.0.clone | all-reduce | flops 128 | bytes 1024
  140.0 0.8 fusion.92
  141.6 2.5 %psum.38 = f32[1,8,128]{2,1,0:T(8,128)S(1)} all-reduce(f32[1,8,128]{2,1,0:T(8,128)S(1)} %add_bitcast_fusion), channel_id=1, replica_groups=mesh['grp'=2,'row'=4,'head'=2,'br'=2] {'br'}, use_global_device_ids=true, to_apply=%region_17.0 | all-reduce | flops 1024 | bytes 8192 | tf_op jit(solution)/shard_map/psum | solution.py:20
  144.6 3.3 %all-to-all-start.3 = ((f32[8,1,128]{2,1,0:T(1,128)}), f32[8,1,128]{2,1,0:T(1,128)S(1)}, u32[]{:S(2)}, u32[]{:S(2)}) async-start(f32[8,1,128]{2,1,0:T(1,128)} %bitcast.75), calls=%async_computation.3 | async-start | bytes 8192 | tf_op jit(solution)/shard_map/all_to_all | solution.py:25
  148.2 6.1 %all-to-all-done.3 = f32[8,1,128]{2,1,0:T(1,128)S(1)} async-done(((f32[8,1,128]{2,1,0:T(1,128)}), f32[8,1,128]{2,1,0:T(1,128)S(1)}, u32[]{:S(2)}, u32[]{:S(2)}) %all-to-all-start.3) | async-done | bytes 4128 | tf_op jit(solution)/shard_map/all_to_all | solution.py:25
  155.6 17.9 %all-reduce.9 = f32[2,8,8]{2,0,1:T(2,128)S(1)} all-reduce(f32[2,8,8]{2,0,1:T(2,128)S(1)} %copy.52), channel_id=5, replica_groups=mesh['grp'=2,'row'=4,'head'=2,'br'=2] {'row','head'}, use_global_device_ids=true, to_apply=%region_19.0.clone | all-reduce | flops 128 | bytes 1024
  173.5 0.8 fusion.91
  175.1 2.5 %all-reduce.10 = (f32[1,8,128]{2,1,0:T(8,128)S(1)}, f32[1,8,128]{2,1,0:T(8,128)S(1)}) all-reduce(f32[1,8,128]{2,1,0:T(8,128)S(1)} %convolution_bitcast_fusion.15, f32[1,8,128]{2,1,0:T(8,128)S(1)} %broadcast_add_fusion), channel_id=1, replica_groups=mesh['grp'=2,'row'=4,'head'=2,'br'=2] {'br'}, use_global_device_ids=true, to_apply=%region_12.0 | all-reduce | flops 2048 | bytes 16384 | tf_op jit(solution)/shard_map/psum | solution.py:20
  178.2 3.3 %all-to-all-start.1 = ((f32[8,1,128]{2,1,0:T(1,128)}), f32[8,1,128]{2,1,0:T(1,128)S(1)}, u32[]{:S(2)}, u32[]{:S(2)}) async-start(f32[8,1,128]{2,1,0:T(1,128)} %bitcast.52), calls=%async_computation.1 | async-start | bytes 8192 | tf_op jit(solution)/shard_map/all_to_all | solution.py:25
  182.1 5.8 %all-to-all-done.1 = f32[8,1,128]{2,1,0:T(1,128)S(1)} async-done(((f32[8,1,128]{2,1,0:T(1,128)}), f32[8,1,128]{2,1,0:T(1,128)S(1)}, u32[]{:S(2)}, u32[]{:S(2)}) %all-to-all-start.1) | async-done | bytes 4128 | tf_op jit(solution)/shard_map/all_to_all | solution.py:25
  (101 shorter events, 16.6 us)
Async XLA Ops:
  0.6 35.6 %copy-start = (f32[1024,128]{1,0:T(8,128)S(1)}, f32[1024,128]{1,0:T(8,128)}, u32[]{:S(2)}) copy-start(f32[1024,128]{1,0:T(8,128)} %param.18) | copy-start | bytes 1572868
  0.6 1.0 copy-start.3
  0.7 2.8 %copy-start.4 = (f32[256,64]{0,1:T(8,128)S(1)}, f32[256,64]{0,1:T(8,128)}, u32[]{:S(2)}) copy-start(f32[256,64]{0,1:T(8,128)} %param.17) | copy-start | bytes 196612
  36.9 24.4 %copy-start.1 = (f32[2,128,2,128]{3,2,1,0:T(2,128)S(1)}, f32[2,128,2,128]{3,2,1,0:T(2,128)}, u32[]{:S(2)}) copy-start(f32[2,128,2,128]{3,2,1,0:T(2,128)} %param.20) | copy-start | bytes 786436
  60.5 0.7 copy-start.8
  61.2 0.7 copy-start.7
  61.2 0.7 copy-start.6
  62.3 0.7 copy-start.9
  64.2 0.7 copy-start.5
  81.7 0.8 copy-start.2
  85.9 9.7 %all-to-all-start = ((f32[8,1,128]{2,1,0:T(1,128)}), f32[8,1,128]{2,1,0:T(1,128)S(1)}, u32[]{:S(2)}, u32[]{:S(2)}) async-start(f32[8,1,128]{2,1,0:T(1,128)} %bitcast.32), calls=%async_computation | async-start | bytes 8192 | tf_op jit(solution)/shard_map/all_to_all | solution.py:25
  89.2 0.7 copy-start.10
  95.6 25.7 %all-to-all-start.2 = ((f32[8,1,128]{2,1,0:T(1,128)}), f32[8,1,128]{2,1,0:T(1,128)S(1)}, u32[]{:S(2)}, u32[]{:S(2)}) async-start(f32[8,1,128]{2,1,0:T(1,128)} %bitcast.54), calls=%async_computation.2 | async-start | bytes 8192 | tf_op jit(solution)/shard_map/all_to_all | solution.py:25
  144.6 9.7 %all-to-all-start.3 = ((f32[8,1,128]{2,1,0:T(1,128)}), f32[8,1,128]{2,1,0:T(1,128)S(1)}, u32[]{:S(2)}, u32[]{:S(2)}) async-start(f32[8,1,128]{2,1,0:T(1,128)} %bitcast.75), calls=%async_computation.3 | async-start | bytes 8192 | tf_op jit(solution)/shard_map/all_to_all | solution.py:25
  178.2 9.7 %all-to-all-start.1 = ((f32[8,1,128]{2,1,0:T(1,128)}), f32[8,1,128]{2,1,0:T(1,128)S(1)}, u32[]{:S(2)}, u32[]{:S(2)}) async-start(f32[8,1,128]{2,1,0:T(1,128)} %bitcast.52), calls=%async_computation.1 | async-start | bytes 8192 | tf_op jit(solution)/shard_map/all_to_all | solution.py:25
where the time goes:
time: 189 us; the launch traced here: 188 us
  blocking collectives  135 us (71%)
  waiting for transfers between devices  17 us (9%)
  starting transfers between devices  13.2 us (7%)
  matrix products  8.39 us (4%)
  other arithmetic  7.59 us (4%)
  local copies, waits for them, and re-layouts  6.07 us (3%)
    all_gather x2, blocking collectives, tri_forward(): bias_full = lax.all_gather(bias_local, ('row', 'head'), axis=1, tiled=True)  37.2 us
    unnamed x2, blocking collectives  35.3 us
    all_gather x1, blocking collectives, body(): lax.all_gather(right_part, ('row', 'head'), axis=2, tiled=True)  32.3 us
    all_gather x1, blocking collectives, body(): lax.all_gather(mask_all, ('row', 'head'), axis=1, tiled=True)  20.4 us
    all_to_all x4, waiting for transfers between devices, reorient(): lax.all_to_all(turned, ('row', 'head'), split_axis=0, concat_axis=1, tile...  17 us
    all_to_all x4, starting transfers between devices, reorient(): lax.all_to_all(turned, ('row', 'head'), split_axis=0, concat_axis=1, tile...  13.2 us
    psum x4, blocking collectives, core_total(): return lax.psum(values, 'br')  9.82 us
    unnamed x26, local copies, waits for them, and re-layouts  4.8 us
  transfers between devices with their start and end apart: 4, of which 3 were waited for; matrix products, arithmetic and copies ran while one was open for 2% of the time, Pallas kernels for 0%

commit v1 on v0

--- a/solution.py
+++ b/solution.py
@@ -54,7 +54,10 @@
         return prepare(values, scales, weight_in, weight_bias)
 
     (projected, bias_local), pull_prep = jax.vjp(local_prep, rows_in)
-    bias_full = lax.all_gather(bias_local, ("row", "head"), axis=1, tiled=True)
+    size = lax.axis_size(("row", "head"))
+    blocks = jnp.stack([bias_local for _ in range(size)])
+    blocks = lax.all_to_all(blocks, ("row", "head"), split_axis=0, concat_axis=0)
+    bias_full = jnp.concatenate(blocks, axis=1)
 
     def local_attend(proj_in, bias_in):
         return attend(proj_in, bias_in, key_shift, weight_out)

time: 189 us -> 173 us (0.915)
  blocking collectives: 135 us -> 98.5 us
  waiting for transfers between devices: 17 us -> 29.6 us
  starting transfers between devices: 13.2 us -> 20.5 us
    all_gather x2 -> x0, blocking collectives: 37.2 us -> none  [tri_forward(): bias_full = lax.all_gather(bias_local, ('row', 'head'), axis=1, tiled=True)]
    all_to_all x0 -> x2, waiting for transfers between devices: none -> 9.38 us  [tri_forward(): lax.all_to_all(blocks, ('row', 'head'), split_axis=0, concat_axis=0)]
    all_to_all x0 -> x2, starting transfers between devices: none -> 6.66 us  [tri_forward(): lax.all_to_all(blocks, ('row', 'head'), split_axis=0, concat_axis=0)]
    all_to_all x4, waiting for transfers between devices: 17 us -> 20.2 us  [reorient(): lax.all_to_all(turned, ('row', 'head'), split_axis=0, concat_axis=1, tile...]
    unnamed x26 -> x24, local copies, waits for them, and re-layouts: 4.8 us -> 4.1 us
  transfers between devices with their start and end apart: 4 -> 6, of which waited for: 3 -> 6; matrix products, arithmetic and copies ran while one was open for 2% -> 3% of each run, Pallas kernels for 0% -> 0%
where the time goes in v1:
time: 173 us; the launch traced here: 172 us
  blocking collectives  98.5 us (57%)
  waiting for transfers between devices  29.6 us (17%)
  starting transfers between devices  20.5 us (12%)
  matrix products  8.35 us (5%)
  other arithmetic  7.58 us (4%)
  local copies, waits for them, and re-layouts  6.44 us (4%)
    unnamed x2, blocking collectives  35.8 us
    all_gather x1, blocking collectives, body(): lax.all_gather(right_part, ('row', 'head'), axis=2, tiled=True)  32.3 us
    all_gather x1, blocking collectives, body(): lax.all_gather(mask_all, ('row', 'head'), axis=1, tiled=True)  20.4 us
    all_to_all x4, waiting for transfers between devices, reorient(): lax.all_to_all(turned, ('row', 'head'), split_axis=0, concat_axis=1, tile...  20.2 us
    all_to_all x4, starting transfers between devices, reorient(): lax.all_to_all(turned, ('row', 'head'), split_axis=0, concat_axis=1, tile...  13.8 us
    psum x4, blocking collectives, core_total(): return lax.psum(values, 'br')  9.82 us
    all_to_all x2, waiting for transfers between devices, tri_forward(): lax.all_to_all(blocks, ('row', 'head'), split_axis=0, concat_axis=0)  9.38 us
    all_to_all x2, starting transfers between devices, tri_forward(): lax.all_to_all(blocks, ('row', 'head'), split_axis=0, concat_axis=0)  6.66 us
  transfers between devices with their start and end apart: 6, of which 6 were waited for; matrix products, arithmetic and copies ran while one was open for 3% of the time, Pallas kernels for 0%

profile of v1, /device:TPU:0, one launch (start us, length us, event | category | flops | bytes accessed | tf_op | source)
XLA Modules:
  0.0 171.9 jit_solution(11429963420560062672)
XLA Ops:
  0.7 1.0 reduce_sum.121
  2.6 0.8 multiply_multiply_fusion
  3.7 32.3 %all_gather.6 = f32[16,32,8]{1,0,2:T(8,128)S(1)} all-gather(f32[16,32,1]{1,0,2:T(8,128)S(1)} %fusion.30), channel_id=1, replica_groups=mesh['grp'=2,'row'=4,'head'=2,'br'=2] {'row','head'}, dimensions={2}, use_global_device_ids=true | all-gather | bytes 18432 | tf_op jit(solution)/shard_map/all_gather | solution.py:107
  37.6 2.5 %psum.35 = f32[1,8,128]{2,1,0:T(8,128)S(1)} all-reduce(f32[1,8,128]{2,1,0:T(8,128)S(1)} %convolution_bitcast_fusion.17), channel_id=1, replica_groups=mesh['grp'=2,'row'=4,'head'=2,'br'=2] {'br'}, use_global_device_ids=true, to_apply=%region_2.0 | all-reduce | flops 1024 | bytes 8192 | tf_op jit(solution)/shard_map/psum | solution.py:20
  40.0 20.4 %all-gather = f32[8,1,32]{2,1,0:T(1,128)S(1)} all-gather(f32[1,1,32]{2,1,0:T(1,128)S(1)} %get-tuple-element.16), channel_id=1, replica_groups=mesh['grp'=2,'row'=4,'head'=2,'br'=2] {'row','head'}, dimensions={0}, use_global_device_ids=true | all-gather | bytes 1152 | tf_op jit(solution)/shard_map/all_gather | solution.py:108
  63.0 3.3 %all-to-all-start = ((f32[8,2,1,8]{3,1,2,0:T(2,128)}), f32[8,2,1,8]{3,1,2,0:T(2,128)S(1)}, u32[]{:S(2)}, u32[]{:S(2)}) async-start(f32[8,2,1,8]{3,1,2,0:T(2,128)} %stack.4), calls=%async_computation | async-start | bytes 16384 | tf_op jit(solution)/shard_map/all_to_all | solution.py:59
  69.8 3.1 %all-to-all-done = f32[8,2,1,8]{3,1,2,0:T(2,128)S(1)} async-done(((f32[8,2,1,8]{3,1,2,0:T(2,128)}), f32[8,2,1,8]{3,1,2,0:T(2,128)S(1)}, u32[]{:S(2)}, u32[]{:S(2)}) %all-to-all-start) | async-done | bytes 544 | tf_op jit(solution)/shard_map/all_to_all | solution.py:59
  72.8 3.3 %all-to-all-start.4 = ((f32[8,1,128]{2,1,0:T(1,128)}), f32[8,1,128]{2,1,0:T(1,128)S(1)}, u32[]{:S(2)}, u32[]{:S(2)}) async-start(f32[8,1,128]{2,1,0:T(1,128)} %bitcast.58), calls=%async_computation.4 | async-start | bytes 8192 | tf_op jit(solution)/shard_map/all_to_all | solution.py:25
  77.4 2.5 %psum.36 = f32[1,8,128]{2,1,0:T(8,128)S(1)} all-reduce(f32[1,8,128]{2,1,0:T(8,128)S(1)} %convolution_bitcast_fusion.16), channel_id=1, replica_groups=mesh['grp'=2,'row'=4,'head'=2,'br'=2] {'br'}, use_global_device_ids=true, to_apply=%region_7.0 | all-reduce | flops 1024 | bytes 8192 | tf_op jit(solution)/shard_map/psum | solution.py:20
  80.5 2.0 %all-to-all-done.4 = f32[8,1,128]{2,1,0:T(1,128)S(1)} async-done(((f32[8,1,128]{2,1,0:T(1,128)}), f32[8,1,128]{2,1,0:T(1,128)S(1)}, u32[]{:S(2)}, u32[]{:S(2)}) %all-to-all-start.4) | async-done | bytes 4128 | tf_op jit(solution)/shard_map/all_to_all | solution.py:25
  82.5 3.9 %all-to-all-start.1 = ((f32[8,1,128]{2,1,0:T(1,128)}), f32[8,1,128]{2,1,0:T(1,128)S(1)}, u32[]{:S(2)}, u32[]{:S(2)}) async-start(f32[8,1,128]{2,1,0:T(1,128)} %bitcast.34), calls=%async_computation.1 | async-start | bytes 8192 | tf_op jit(solution)/shard_map/all_to_all | solution.py:25
  86.5 6.3 %all-to-all-done.1 = f32[8,1,128]{2,1,0:T(1,128)S(1)} async-done(((f32[8,1,128]{2,1,0:T(1,128)}), f32[8,1,128]{2,1,0:T(1,128)S(1)}, u32[]{:S(2)}, u32[]{:S(2)}) %all-to-all-start.1) | async-done | bytes 4128 | tf_op jit(solution)/shard_map/all_to_all | solution.py:25
  94.0 3.3 %all-to-all-start.2 = ((f32[8,2,1,8]{3,1,2,0:T(2,128)}), f32[8,2,1,8]{3,1,2,0:T(2,128)S(1)}, u32[]{:S(2)}, u32[]{:S(2)}) async-start(f32[8,2,1,8]{3,1,2,0:T(2,128)} %stack.5), calls=%async_computation.2 | async-start | bytes 16384 | tf_op jit(solution)/shard_map/all_to_all | solution.py:59
  97.5 6.3 %all-to-all-done.2 = f32[8,2,1,8]{3,1,2,0:T(2,128)S(1)} async-done(((f32[8,2,1,8]{3,1,2,0:T(2,128)}), f32[8,2,1,8]{3,1,2,0:T(2,128)S(1)}, u32[]{:S(2)}, u32[]{:S(2)}) %all-to-all-start.2) | async-done | bytes 544 | tf_op jit(solution)/shard_map/all_to_all | solution.py:59
  105.6 17.9 %all-reduce.8 = f32[2,8,8]{2,0,1:T(2,128)S(1)} all-reduce(f32[2,8,8]{2,0,1:T(2,128)S(1)} %copy.45), channel_id=2, replica_groups=mesh['grp'=2,'row'=4,'head'=2,'br'=2] {'row','head'}, use_global_device_ids=true, to_apply=%region_14.0.clone | all-reduce | flops 128 | bytes 1024
  123.5 0.8 fusion.92
  125.0 2.5 %psum.38 = f32[1,8,128]{2,1,0:T(8,128)S(1)} all-reduce(f32[1,8,128]{2,1,0:T(8,128)S(1)} %add_bitcast_fusion), channel_id=1, replica_groups=mesh['grp'=2,'row'=4,'head'=2,'br'=2] {'br'}, use_global_device_ids=true, to_apply=%region_17.0 | all-reduce | flops 1024 | bytes 8192 | tf_op jit(solution)/shard_map/psum | solution.py:20
  128.1 3.3 %all-to-all-start.5 = ((f32[8,1,128]{2,1,0:T(1,128)}), f32[8,1,128]{2,1,0:T(1,128)S(1)}, u32[]{:S(2)}, u32[]{:S(2)}) async-start(f32[8,1,128]{2,1,0:T(1,128)} %bitcast.79), calls=%async_computation.5 | async-start | bytes 8192 | tf_op jit(solution)/shard_map/all_to_all | solution.py:25
  131.7 6.1 %all-to-all-done.5 = f32[8,1,128]{2,1,0:T(1,128)S(1)} async-done(((f32[8,1,128]{2,1,0:T(1,128)}), f32[8,1,128]{2,1,0:T(1,128)S(1)}, u32[]{:S(2)}, u32[]{:S(2)}) %all-to-all-start.5) | async-done | bytes 4128 | tf_op jit(solution)/shard_map/all_to_all | solution.py:25
  139.0 17.9 %all-reduce.9 = f32[2,8,8]{2,0,1:T(2,128)S(1)} all-reduce(f32[2,8,8]{2,0,1:T(2,128)S(1)} %copy.48), channel_id=3, replica_groups=mesh['grp'=2,'row'=4,'head'=2,'br'=2] {'row','head'}, use_global_device_ids=true, to_apply=%region_19.0.clone | all-reduce | flops 128 | bytes 1024
  157.0 0.8 fusion.91
  158.5 2.5 %all-reduce.10 = (f32[1,8,128]{2,1,0:T(8,128)S(1)}, f32[1,8,128]{2,1,0:T(8,128)S(1)}) all-reduce(f32[1,8,128]{2,1,0:T(8,128)S(1)} %convolution_bitcast_fusion.15, f32[1,8,128]{2,1,0:T(8,128)S(1)} %broadcast_add_fusion), channel_id=1, replica_groups=mesh['grp'=2,'row'=4,'head'=2,'br'=2] {'br'}, use_global_device_ids=true, to_apply=%region_12.0 | all-reduce | flops 2048 | bytes 16384 | tf_op jit(solution)/shard_map/psum | solution.py:20
  161.6 3.3 %all-to-all-start.3 = ((f32[8,1,128]{2,1,0:T(1,128)}), f32[8,1,128]{2,1,0:T(1,128)S(1)}, u32[]{:S(2)}, u32[]{:S(2)}) async-start(f32[8,1,128]{2,1,0:T(1,128)} %bitcast.56), calls=%async_computation.3 | async-start | bytes 8192 | tf_op jit(solution)/shard_map/all_to_all | solution.py:25
  165.5 5.8 %all-to-all-done.3 = f32[8,1,128]{2,1,0:T(1,128)S(1)} async-done(((f32[8,1,128]{2,1,0:T(1,128)}), f32[8,1,128]{2,1,0:T(1,128)S(1)}, u32[]{:S(2)}, u32[]{:S(2)}) %all-to-all-start.3) | async-done | bytes 4128 | tf_op jit(solution)/shard_map/all_to_all | solution.py:25
  (99 shorter events, 18.9 us)
Async XLA Ops:
  0.6 35.6 %copy-start = (f32[1024,128]{1,0:T(8,128)S(1)}, f32[1024,128]{1,0:T(8,128)}, u32[]{:S(2)}) copy-start(f32[1024,128]{1,0:T(8,128)} %param.18) | copy-start | bytes 1572868
  0.6 1.0 copy-start.3
  0.7 2.8 %copy-start.4 = (f32[256,64]{0,1:T(8,128)S(1)}, f32[256,64]{0,1:T(8,128)}, u32[]{:S(2)}) copy-start(f32[256,64]{0,1:T(8,128)} %param.17) | copy-start | bytes 196612
  36.9 23.6 %copy-start.8 = (s32[32,1]{0,1:T(1,128)S(1)}, s32[32,1]{0,1:T(1,128)}, u32[]{:S(2)}) copy-start(s32[32,1]{0,1:T(1,128)} %param.14) | copy-start | bytes 388
  36.9 29.5 %copy-start.1 = (f32[2,128,2,128]{3,2,1,0:T(2,128)S(1)}, f32[2,128,2,128]{3,2,1,0:T(2,128)}, u32[]{:S(2)}) copy-start(f32[2,128,2,128]{3,2,1,0:T(2,128)} %param.20) | copy-start | bytes 786436
  60.5 0.7 copy-start.6
  60.5 0.7 copy-start.7
  61.5 0.7 copy-start.5
  63.0 9.8 %all-to-all-start = ((f32[8,2,1,8]{3,1,2,0:T(2,128)}), f32[8,2,1,8]{3,1,2,0:T(2,128)S(1)}, u32[]{:S(2)}, u32[]{:S(2)}) async-start(f32[8,2,1,8]{3,1,2,0:T(2,128)} %stack.4), calls=%async_computation | async-start | bytes 16384 | tf_op jit(solution)/shard_map/all_to_all | solution.py:59
  66.4 0.7 copy-start.9
  68.5 0.7 copy-start.10
  72.8 9.7 %all-to-all-start.4 = ((f32[8,1,128]{2,1,0:T(1,128)}), f32[8,1,128]{2,1,0:T(1,128)S(1)}, u32[]{:S(2)}, u32[]{:S(2)}) async-start(f32[8,1,128]{2,1,0:T(1,128)} %bitcast.58), calls=%async_computation.4 | async-start | bytes 8192 | tf_op jit(solution)/shard_map/all_to_all | solution.py:25
  76.2 0.8 copy-start.2
  82.5 10.3 %all-to-all-start.1 = ((f32[8,1,128]{2,1,0:T(1,128)}), f32[8,1,128]{2,1,0:T(1,128)S(1)}, u32[]{:S(2)}, u32[]{:S(2)}) async-start(f32[8,1,128]{2,1,0:T(1,128)} %bitcast.34), calls=%async_computation.1 | async-start | bytes 8192 | tf_op jit(solution)/shard_map/all_to_all | solution.py:25
  94.0 9.8 %all-to-all-start.2 = ((f32[8,2,1,8]{3,1,2,0:T(2,128)}), f32[8,2,1,8]{3,1,2,0:T(2,128)S(1)}, u32[]{:S(2)}, u32[]{:S(2)}) async-start(f32[8,2,1,8]{3,1,2,0:T(2,128)} %stack.5), calls=%async_computation.2 | async-start | bytes 16384 | tf_op jit(solution)/shard_map/all_to_all | solution.py:59
  128.1 9.7 %all-to-all-start.5 = ((f32[8,1,128]{2,1,0:T(1,128)}), f32[8,1,128]{2,1,0:T(1,128)S(1)}, u32[]{:S(2)}, u32[]{:S(2)}) async-start(f32[8,1,128]{2,1,0:T(1,128)} %bitcast.79), calls=%async_computation.5 | async-start | bytes 8192 | tf_op jit(solution)/shard_map/all_to_all | solution.py:25
  161.6 9.7 %all-to-all-start.3 = ((f32[8,1,128]{2,1,0:T(1,128)}), f32[8,1,128]{2,1,0:T(1,128)S(1)}, u32[]{:S(2)}, u32[]{:S(2)}) async-start(f32[8,1,128]{2,1,0:T(1,128)} %bitcast.56), calls=%async_computation.3 | async-start | bytes 8192 | tf_op jit(solution)/shard_map/all_to_all | solution.py:25
